TPU v7x, 32 devices: a whole 2x2x4 slice. The times are simulated.
32 devices in a mesh: expert: 8 (over z, x), dp: 4 (over y, core).
Axes of the slice: x: 2, y: 2, z: 4, core: 2. Of those that a mesh axis runs over, the one named last changes fastest.
Arguments:
- sub_inputs: bfloat16 [4096, 4096], P(('expert', 'dp')), may hold values from -6 to 6
- out_grads: bfloat16 [4096, 4096], P(('expert', 'dp')), may hold values from -6 to 6
- expert_outputs: bfloat16 [4096, 4, 2, 1024], P(('expert', 'dp')), may hold values from -6 to 6
- combine_weights: float32 [4096, 4, 2], P(('expert', 'dp')), may hold values from 0.1 to 1
- expert_ids: int32 [4096, 4, 2], P(('expert', 'dp')), may hold values from 0 to 7, as said below
- slot_ids: int32 [4096, 4, 2], P(('expert', 'dp')), may hold values from -1 to 127, as said below
- expert_input_weight: bfloat16 [8, 1024, 1024], P('expert'), may hold values from -0.1875 to 0.1875
- expert_output_weight: bfloat16 [8, 1024, 1024], P('expert'), may hold values from -0.1875 to 0.1875
Outputs:
- d_inputs: bfloat16 [4096, 4096], P(('expert', 'dp'))
- d_gates: float32 [4096, 4, 2], P(('expert', 'dp'))
- dw_in: float32 [8, 1024, 1024], P('expert', 'dp')
- dw_out: float32 [8, 1024, 1024], P('expert', 'dp')
Inputs may be any that keep to these rules, and one draw needn't show every extreme that they name: `expert_ids`: the 2 experts of one sub-token differ. `slot_ids`: within the rows of one device, the kept entries that name one expert carry the slots 0, 1, 2, ... each once, so at most 128 of them; in every draw some expert has 128 kept entries from every device.
All inputs are finite; a program needn't handle non-finite values.
Results may differ from a plain program's by a relative error of at most 0.0085.
Values may be sent and summed in bfloat16 or wider, within the bound.
A program may use at most 128 MiB of HBM per device.

v0:
```python
import functools

import jax
import jax.numpy as jnp
from jax import lax
from jax.experimental import pallas as pl
from jax.experimental.pallas import tpu as pltpu
from jax.sharding import PartitionSpec as P

MESH = pl.DeviceIdType.MESH
F32 = jnp.float32
BF16 = jnp.bfloat16
ROOT = 0.7978845608028654
CUBE = 0.044715


def partner(me, step, count):
    if count & (count - 1):
        return lax.rem(step - me + count, count)
    out, bit = 0, 1
    while bit < count:
        out = out + ((me // bit + step // bit) % 2) * bit
        bit *= 2
    return out


def spread(i, count):
    return lax.rem(i + 1, count)


def dot(a, b, ca, cb):
    return lax.dot_general(a, b, (((ca,), (cb,)), ((), ())), preferred_element_type=F32)


def kernel(
    dims,
    tgt, cw, x_hbm, g_hbm, win_hbm, wout_hbm, eo_hbm,
    dx, dwi, dwo, dg,
    xs, gs, win, wout, sx, sg, rx, rg, rs, rr, hb, fb, acc, po, pi, tpo, tpi, so, si, rpo, rpi,
    ev, load_sem, xg_send, xg_recv, r_send, r_recv, t_send, t_recv, w_send, w_recv,
):
    groups, replicas, cap, heads, tokens, sub, ff = dims
    chunk = max(cap, 128)
    per = chunk // cap
    chunks = groups * cap // chunk
    tile = 256
    me = lax.axis_index("expert")
    mine = lax.axis_index("dp")
    my_chunk = me // per
    halves = replicas // 2
    row, side = mine // 2, mine % 2
    twin = row * 2 + (1 - side)

    loads = []
    for h in range(heads):
        for s, (src, dst) in enumerate(((x_hbm, xs), (g_hbm, gs))):
            loads.append(
                pltpu.make_async_copy(
                    src.at[:, pl.ds(h * sub, sub)], dst.at[pl.ds(h * tokens, tokens)], load_sem.at[2 * h + s]
                )
            )
    wloads = [
        pltpu.make_async_copy(win_hbm.at[0], win, load_sem.at[2 * heads]),
        pltpu.make_async_copy(wout_hbm.at[0], wout, load_sem.at[2 * heads + 1]),
        pltpu.make_async_copy(eo_hbm, ev, load_sem.at[2 * heads + 2]),
    ]
    for c in loads + wloads:
        c.start()

    barrier = pltpu.get_barrier_semaphore()

    @pl.loop(1, groups)
    def _(i):
        pl.semaphore_signal(barrier, inc=1, device_id={"expert": lax.rem(me + i, groups)}, device_id_type=MESH)

    @pl.loop(1, replicas)
    def _(i):
        pl.semaphore_signal(barrier, inc=1, device_id={"dp": lax.rem(mine + i, replicas)}, device_id_type=MESH)

    pl.semaphore_wait(barrier, groups + replicas - 2)
    for c in loads:
        c.wait()

    def rows_of(index, size):
        return pl.ds(pl.multiple_of(index * size, size), size)

    def hot(j):
        slots = lax.broadcasted_iota(jnp.int32, (chunk, tgt.shape[1]), 0) + j * chunk
        return tgt[0:1, :] == slots, tgt[1:2, :] == slots

    def xg_copy(s, peer):
        src, dst = ((sx, rx), (sg, rg))[s]
        return pltpu.make_async_remote_copy(
            src_ref=src.at[rows_of(peer, cap)], dst_ref=dst.at[rows_of(me, cap)],
            send_sem=xg_send.at[s, peer], recv_sem=xg_recv.at[s, me],
            device_id={"expert": peer}, device_id_type=MESH,
        )

    def xg_local(s, src_dev):
        src, dst = ((sx, rx), (sg, rg))[s]
        return pltpu.make_async_copy(
            src.at[rows_of(src_dev, cap)], dst.at[rows_of(src_dev, cap)], xg_recv.at[s, src_dev]
        )

    def r_copy(peer):
        return pltpu.make_async_remote_copy(
            src_ref=rs.at[rows_of(peer, cap)], dst_ref=rr.at[rows_of(me, cap)],
            send_sem=r_send.at[peer], recv_sem=r_recv.at[me],
            device_id={"expert": peer}, device_id_type=MESH,
        )

    def r_local(src_dev):
        return pltpu.make_async_copy(
            rs.at[rows_of(src_dev, cap)], rr.at[rows_of(src_dev, cap)], r_recv.at[src_dev]
        )

    def twin_copy(s, q, t):
        src, dst = ((po, tpo), (pi, tpi))[s]
        return pltpu.make_async_remote_copy(
            src_ref=src.at[q], dst_ref=dst.at[t],
            send_sem=t_send.at[s, t], recv_sem=t_recv.at[s, t],
            device_id={"dp": twin}, device_id_type=MESH,
        )

    def row_copy(s, t):
        src, dst = ((so, rpo), (si, rpi))[s]
        return pltpu.make_async_remote_copy(
            src_ref=src.at[t], dst_ref=dst.at[row],
            send_sem=w_send.at[s, t], recv_sem=w_recv.at[s, row],
            device_id={"dp": 2 * t + side}, device_id_type=MESH,
        )

    def row_got(s, t):
        dst = (rpo, rpi)[s]
        return pltpu.make_async_copy(dst.at[t], dst.at[t], w_recv.at[s, t])

    @pl.loop(0, chunks)
    def _(i):
        j = partner(my_chunk, spread(i, chunks), chunks)
        h0, h1 = hot(j)
        one = (h0 | h1).astype(F32).astype(BF16)
        w = jnp.sum(jnp.where(h0, cw[0:1, :], 0.0) + jnp.where(h1, cw[1:2, :], 0.0), axis=1, keepdims=True)
        sx[rows_of(j, chunk), :] = dot(one, xs[...], 1, 0).astype(BF16)
        sg[rows_of(j, chunk), :] = (dot(one, gs[...], 1, 0) * w).astype(BF16)
        for p in range(per):
            peer = j * per + p

            @pl.when(peer != me)
            def _():
                xg_copy(0, peer).start()
                xg_copy(1, peer).start()

            @pl.when(peer == me)
            def _():
                xg_local(0, me).start()
                xg_local(1, me).start()

    for c in wloads:
        c.wait()

    span = 16
    for h in range(heads):

        @pl.loop(0, tokens // span)
        def _(b):
            grads = gs[rows_of(h * (tokens // span) + b, span), :].astype(F32)
            terms = ev[rows_of(b, span), h].astype(F32) * grads[:, None, :]
            dg[h, rows_of(b, span), :] = jnp.sum(terms, axis=-1)

    @pl.loop(0, chunks)
    def _(i):
        j = partner(my_chunk, spread(lax.rem(i + chunks - 1, chunks), chunks), chunks)
        for p in range(per):
            xg_local(0, j * per + p).wait()
            xg_local(1, j * per + p).wait()
        rows = rows_of(j, chunk)
        for n in range(ff // tile):
            cols = pl.ds(n * tile, tile)
            z = dot(rx[rows, :], win[:, cols], 1, 0)
            e = dot(rg[rows, :], wout[cols, :], 1, 1)
            zz = z * z
            t = jnp.tanh(ROOT * (z + CUBE * (zz * z)))
            half = 0.5 * (1.0 + t)
            hb[rows, cols] = (z * half).astype(BF16)
            slope = half + 0.5 * z * (1.0 - t * t) * (ROOT * (1.0 + 3.0 * CUBE * zz))
            fb[rows, cols] = (e * slope).astype(BF16)
        for n in range(sub // tile):
            cols = pl.ds(n * tile, tile)
            rs[rows, cols] = dot(fb[rows, :], win[cols, :], 1, 1).astype(BF16)
        for p in range(per):
            peer = j * per + p

            @pl.when(peer != me)
            def _():
                r_copy(peer).start()

            @pl.when(peer == me)
            def _():
                r_local(me).start()

    block = dwo.shape[1]
    def product(q):
        cols = rows_of(q, block)
        po[q] = dot(hb[:, cols], rg[...], 0, 0).astype(BF16)
        pi[q] = dot(rx[:, cols], fb[...], 0, 0).astype(BF16)

    @pl.loop(0, halves)
    def _(i):
        t = lax.rem(row + 1 + i, halves)
        product(2 * t + (1 - side))
        twin_copy(0, 2 * t + (1 - side), t).start()
        twin_copy(1, 2 * t + (1 - side), t).start()
        product(2 * t + side)

        @pl.when(t != row)
        def _():
            for s, (own, got, out) in enumerate(((po, tpo, so), (pi, tpi, si))):
                twin_copy(s, 2 * t + side, t).wait_recv()
                out[t] = (own[2 * t + side].astype(F32) + got[t].astype(F32)).astype(BF16)
                row_copy(s, t).start()

    acc[...] = jnp.zeros_like(acc)

    @pl.loop(0, chunks)
    def _(i):
        j = partner(my_chunk, spread(lax.rem(i + chunks - 1, chunks), chunks), chunks)
        for p in range(per):
            r_local(j * per + p).wait()
        h0, h1 = hot(j)
        one = (h0 | h1).astype(F32).astype(BF16)
        acc[...] += dot(one, rr[rows_of(j, chunk), :], 0, 0)

    for h in range(heads):
        dx[:, pl.ds(h * sub, sub)] = acc[pl.ds(h * tokens, tokens), :].astype(BF16)

    for s, (out, own, got, sums) in enumerate(((dwo, po, tpo, rpo), (dwi, pi, tpi, rpi))):
        twin_copy(s, mine, row).wait_recv()
        out[0] = own[mine].astype(F32) + got[row].astype(F32)

        @pl.loop(1, halves)
        def _(i):
            t = lax.rem(row + i, halves)
            row_got(s, t).wait()
            out[0] = out[0] + sums[t].astype(F32)

    @pl.loop(1, groups)
    def _(i):
        peer = lax.rem(me + i, groups)
        xg_copy(0, peer).wait_send()
        xg_copy(1, peer).wait_send()
        r_copy(peer).wait_send()

    for s in range(2):

        @pl.loop(0, halves)
        def _(i):
            twin_copy(s, 2 * i + (1 - side), i).wait_send()

        @pl.loop(1, halves)
        def _(i):
            row_copy(s, lax.rem(row + i, halves)).wait_send()


def on_device(
    sub_inputs,
    out_grads,
    expert_outputs,
    combine_weights,
    expert_ids,
    slot_ids,
    expert_input_weight,
    expert_output_weight,
):
    tokens, heads, top = expert_ids.shape
    _, sub, ff = expert_input_weight.shape
    groups = lax.axis_size("expert")
    replicas = lax.axis_size("dp")
    cap = top * heads * tokens // groups
    kept = slot_ids >= 0
    target = jnp.where(kept, expert_ids * cap + slot_ids, -1)
    target = target.transpose(2, 1, 0).reshape(top, heads * tokens)
    weight = combine_weights.transpose(2, 1, 0).reshape(top, heads * tokens)
    slots = groups * cap
    part = sub // replicas
    part_out = ff // replicas
    dims = (groups, replicas, cap, heads, tokens, sub, ff)
    any_spec = pl.BlockSpec(memory_space=pltpu.HBM)
    vmem = pl.BlockSpec(memory_space=pltpu.VMEM)
    dma = pltpu.SemaphoreType.DMA
    d_inputs, dw_in, dw_out, gate_dots = pl.pallas_call(
        functools.partial(kernel, dims),
        out_shape=(
            jax.ShapeDtypeStruct((tokens, heads * sub), BF16),
            jax.ShapeDtypeStruct((1, part, ff), F32),
            jax.ShapeDtypeStruct((1, part_out, sub), F32),
            jax.ShapeDtypeStruct((heads, tokens, top), F32),
        ),
        in_specs=[vmem, vmem, any_spec, any_spec, any_spec, any_spec, any_spec],
        out_specs=(vmem, vmem, vmem, vmem),
        scratch_shapes=[
            pltpu.VMEM((heads * tokens, sub), BF16),
            pltpu.VMEM((heads * tokens, sub), BF16),
            pltpu.VMEM((sub, ff), BF16),
            pltpu.VMEM((ff, sub), BF16),
            pltpu.VMEM((slots, sub), BF16),
            pltpu.VMEM((slots, sub), BF16),
            pltpu.VMEM((slots, sub), BF16),
            pltpu.VMEM((slots, sub), BF16),
            pltpu.VMEM((slots, sub), BF16),
            pltpu.VMEM((slots, sub), BF16),
            pltpu.VMEM((slots, ff), BF16),
            pltpu.VMEM((slots, ff), BF16),
            pltpu.VMEM((heads * tokens, sub), F32),
            pltpu.VMEM((replicas, part_out, sub), BF16),
            pltpu.VMEM((replicas, part, ff), BF16),
            *[pltpu.VMEM((replicas // 2, part_out, sub), BF16), pltpu.VMEM((replicas // 2, part, ff), BF16)] * 3,
            pltpu.VMEM((tokens, heads, top, sub), BF16),
            dma((2 * heads + 3,)),
            dma((2, groups)),
            dma((2, groups)),
            dma((groups,)),
            dma((groups,)),
            *[dma((2, replicas // 2))] * 4,
        ],
        compiler_params=pltpu.CompilerParams(
            collective_id=0, has_side_effects=True, vmem_limit_bytes=60 * 1024 * 1024
        ),
        cost_estimate=pl.CostEstimate(flops=20 * 10**9, bytes_accessed=2**24, transcendentals=0),
    )(target, weight, sub_inputs, out_grads, expert_input_weight, expert_output_weight, expert_outputs)
    d_gates = jnp.where(kept, gate_dots.transpose(1, 0, 2), jnp.float32(0.0))
    return (d_inputs, d_gates, dw_in, dw_out)


def solution(mesh):
    rows = P(("expert", "dp"), None)
    table = P(("expert", "dp"), None, None)
    return jax.shard_map(
        on_device,
        mesh=mesh,
        in_specs=(
            rows,
            rows,
            P(("expert", "dp"), None, None, None),
            table,
            table,
            table,
            P("expert", None, None),
            P("expert", None, None),
        ),
        out_specs=(rows, table, P("expert", "dp", None), P("expert", "dp", None)),
        check_vma=False,
    )
```

profile of v0, /device:TPU:9, one launch (start us, length us, event | category | flops | bytes accessed | tf_op | source)
XLA Modules:
  0.0 163.7 jit_solution(17958125668845859798)
XLA Ops:
  0.6 0.7 broadcast_compare_fusion
  1.3 0.2 copy.24
  1.5 0.7 broadcast_multiply_fusion
  2.2 0.1 copy.22
  2.4 0.8 copy.23
  3.3 0.7 copy.28.tgt
  4.0 153.6 %shard_map.111 = (bf16[128,4096]{1,0:T(8,128)(2,1)}, f32[1,256,1024]{2,1,0:T(8,128)}, f32[1,256,1024]{2,1,0:T(8,128)}, f32[4,128,2]{2,1,0:T(8,128)}) custom-call(s32[2,512]{1,0:T(2,128)} %copy.28.tgt, f32[2,512]{1,0:T(2,128)} %bitcast.9, bf16[128,4096]{1,0:T(8,128)(2,1)} %x_hbm.1, bf16[128,4096]{1,0:T(8,128)(2,1)} %g_hbm.1, bf16[1,1024,1024]{2,1,0:T(8,128)(2,1)} %win_hbm.1, ...), custom_call_target="tpu_custom_call" | custom-call | flops 20000000000 | bytes 16777216 | tf_op jit(solution)/shard_map/pallas_call | solution.py:290
  157.5 0.0 copy-start.1
  157.6 1.1 bitcast_select_fusion
  158.6 0.7 copy.27
  159.3 0.0 copy-start
  159.3 2.4 %copy.32 = bf16[128,4096]{1,0:T(8,128)(2,1)} copy(bf16[128,4096]{1,0:T(8,128)(2,1)} %get-tuple-element.24) | data formatting | bytes 2097152
  161.7 0.0 copy-done.1
  161.7 1.0 copy.33
  162.7 0.0 copy-done
  162.7 1.0 copy.34
  (1 shorter events, 0.0 us)
Async XLA Ops:
  157.5 4.2 %copy-start.1 = (f32[1,256,1024]{2,1,0:T(8,128)S(1)}, f32[1,256,1024]{2,1,0:T(8,128)}, u32[]{:S(2)}) copy-start(f32[1,256,1024]{2,1,0:T(8,128)} %get-tuple-element.26) | copy-start | bytes 3145732
  159.3 3.4 %copy-start = (f32[1,256,1024]{2,1,0:T(8,128)S(1)}, f32[1,256,1024]{2,1,0:T(8,128)}, u32[]{:S(2)}) copy-start(f32[1,256,1024]{2,1,0:T(8,128)} %get-tuple-element.27) | copy-start | bytes 3145732
where the time goes:
time: 164 us
  Pallas kernels  154 us (94%)
  local copies, waits for them, and re-layouts  6.91 us (4%)
  other arithmetic  2.49 us (2%)
    pallas_call x1, Pallas kernels, on_device(): pl.pallas_call(functools.partial(kernel, dims), out_shape=(jax.ShapeDtype...  154 us
    unnamed x9, local copies, waits for them, and re-layouts  5.86 us

commit v1 on v0

--- a/solution.py
+++ b/solution.py
@@ -261,7 +261,7 @@
             row_copy(s, lax.rem(row + i, halves)).wait_send()
 
 
-def on_device(
+def plain_call(
     sub_inputs,
     out_grads,
     expert_outputs,
@@ -331,6 +331,434 @@
     return (d_inputs, d_gates, dw_in, dw_out)
 
 
+PIECES = 2
+
+
+def paired(
+    dims,
+    ids, slot, cw, x_hbm, g_hbm, win_hbm, wout_hbm, eo_hbm,
+    dx, dwi, dwo, dg,
+    tgt, xs, gs, win, wout, sx, sg, rx, rg, rs, rr, hb, fb, acc, po, pi, tpo, tpi, so, si, rpo, rpi,
+    cpo, cpi, gpo, gpi, ev, gates,
+    load_sem, xg_send, xg_recv, r_send, r_recv, wz_send, wz_recv, wt_send, wt_recv, wy_send, wy_recv,
+    t_send, t_recv, y_send, y_recv, c_send, c_recv,
+):
+    groups, replicas, cap, heads, tokens, sub, ff = dims
+    tile = 256
+    me = lax.axis_index("expert")
+    mine = lax.axis_index("dp")
+    half = groups // 2
+    halves = replicas // 2
+    low = lax.rem(me, half)
+    base = me - low
+    opposite = lax.rem(me + half, groups)
+    outer = me // half == low // (half // 2)
+    row, side = mine // 2, mine % 2
+    twin = row * 2 + (1 - side)
+    near = range(1, half)
+
+    def rows_of(index, size):
+        return pl.ds(pl.multiple_of(index * size, size), size)
+
+    def fixed(f, s, n=1):
+        return pl.ds((f * half + s) * cap, n * cap)
+
+    def landed(ref, sem):
+        return pltpu.make_async_copy(ref, ref, sem)
+
+    def remote(src, dst, send, recv, where):
+        return pltpu.make_async_remote_copy(
+            src_ref=src, dst_ref=dst, send_sem=send, recv_sem=recv, device_id=where, device_id_type=MESH
+        )
+
+    loads = []
+    for h in range(heads):
+        for s, (src, dst) in enumerate(((x_hbm, xs), (g_hbm, gs))):
+            loads.append(
+                pltpu.make_async_copy(
+                    src.at[:, pl.ds(h * sub, sub)], dst.at[pl.ds(h * tokens, tokens)], load_sem.at[2 * h + s]
+                )
+            )
+    wloads = [
+        pltpu.make_async_copy(win_hbm.at[0], win.at[0], load_sem.at[2 * heads]),
+        pltpu.make_async_copy(wout_hbm.at[0], wout.at[0], load_sem.at[2 * heads + 1]),
+    ]
+    eload = pltpu.make_async_copy(eo_hbm, ev, load_sem.at[2 * heads + 2])
+    for c in loads + wloads + [eload]:
+        c.start()
+
+    barrier = pltpu.get_barrier_semaphore()
+    for s in near:
+        pl.semaphore_signal(
+            barrier, inc=1, device_id={"expert": base + partner(low, s, half)}, device_id_type=MESH
+        )
+    pl.semaphore_signal(barrier, inc=1, device_id={"expert": opposite}, device_id_type=MESH)
+    for i in range(1, replicas):
+        pl.semaphore_signal(barrier, inc=1, device_id={"dp": lax.rem(mine + i, replicas)}, device_id_type=MESH)
+    pl.semaphore_wait(barrier, half + replicas - 1)
+
+    def owner(s):
+        return base + partner(low, s, half)
+
+    def part_of(m, quarter, n):
+        size = (sub, ff)[m] // replicas // PIECES
+        return rows_of(quarter * PIECES + n, size)
+
+    def held(m, quarter, n):
+        return (win, wout)[m].at[1, part_of(m, quarter, n)]
+
+    def w_cross(m, n):
+        return remote(
+            (win_hbm, wout_hbm)[m].at[0, part_of(m, mine, n)], held(m, mine, n),
+            wz_send.at[m, n], wz_recv.at[m, n], {"expert": opposite},
+        )
+
+    def w_twin(m, n, t):
+        ref = held(m, 2 * t + side, n)
+        return remote(ref, ref, wt_send.at[m, n, t], wt_recv.at[m, n, t], {"dp": twin})
+
+    def w_row(m, n, t):
+        ref = held(m, mine, n)
+        return remote(ref, ref, wy_send.at[m, n, t], wy_recv.at[m, n, row], {"dp": 2 * t + side})
+
+    def xg_copy(s, f, step):
+        src, dst = ((sx, rx), (sg, rg))[s]
+        return remote(
+            src.at[fixed(f, step)], dst.at[fixed(f, step)],
+            xg_send.at[s, f, step], xg_recv.at[s, f, step], {"expert": owner(step)},
+        )
+
+    def r_copy(f, step):
+        return remote(
+            rs.at[fixed(f, step)], rr.at[fixed(f, step)],
+            r_send.at[f, step], r_recv.at[f, step], {"expert": owner(step)},
+        )
+
+    def twin_copy(f, s, q, t):
+        src, dst = ((po, tpo), (pi, tpi))[s]
+        return remote(src.at[f, q], dst.at[f, t], t_send.at[f, s, t], t_recv.at[f, s, t], {"dp": twin})
+
+    def row_copy(f, s, t):
+        src, dst = ((so, rpo), (si, rpi))[s]
+        return remote(
+            src.at[f, t], dst.at[f, row], y_send.at[f, s, t], y_recv.at[f, s, row], {"dp": 2 * t + side}
+        )
+
+    def row_got(f, s, t):
+        ref = (rpo, rpi)[s].at[f, t]
+        return landed(ref, y_recv.at[f, s, t])
+
+    def cross_copy(s):
+        src, dst = ((cpo, gpo), (cpi, gpi))[s]
+        return remote(src, dst, c_send.at[s], c_recv.at[s], {"expert": opposite})
+
+    pieces = [(m, n) for m in range(2) for n in range(PIECES)]
+
+    @pl.when(outer)
+    def _():
+        for m, n in pieces:
+            w_cross(m, n).start()
+
+    tgt[...] = jnp.where(slot[...] >= 0, ids[...] * cap + slot[...], -1)
+
+    def hot(f, step):
+        first = lax.rem(owner(step) + f * half, groups) * cap
+        slots = lax.broadcasted_iota(jnp.int32, (cap, tgt.shape[1]), 0) + first
+        return tgt[0:1, :] == slots, tgt[1:2, :] == slots
+
+    def gather(f, step, out_x, out_g):
+        h0, h1 = hot(f, step)
+        one = (h0 | h1).astype(F32).astype(BF16)
+        w = jnp.sum(jnp.where(h0, cw[0:1, :], 0.0) + jnp.where(h1, cw[1:2, :], 0.0), axis=1, keepdims=True)
+        rows = rows_of(f * half + step, cap)
+        out_x[rows, :] = dot(one, xs[...], 1, 0).astype(BF16)
+        out_g[rows, :] = (dot(one, gs[...], 1, 0) * w).astype(BF16)
+
+    for c in loads:
+        c.wait()
+    far_steps = range(half // 2, half)
+    near_steps = range(1, half // 2)
+
+    for f in (1, 0):
+
+        @pl.loop(0, half - 1)
+        def _(i):
+            step = lax.rem(i + half // 2 - 1, half - 1) + 1
+            gather(f, step, sx, sg)
+            if f == 1:
+                xg_copy(0, f, step).start()
+                xg_copy(1, f, step).start()
+            else:
+
+                @pl.when(jnp.logical_or(outer, step < half // 2))
+                def _():
+                    xg_copy(0, f, step).start()
+                    xg_copy(1, f, step).start()
+
+    @pl.loop(0, 2)
+    def _(f):
+        gather(f, 0, rx, rg)
+
+    eload.wait()
+    span = 16
+    lane = lax.broadcasted_iota(jnp.int32, (span, gates.shape[1]), 1)
+
+    @pl.loop(0, tokens // span)
+    def _(b):
+        found = jnp.zeros((span, gates.shape[1]), F32)
+        for h in range(heads):
+            grads = gs[rows_of(h * (tokens // span) + b, span), :].astype(F32)
+            terms = ev[rows_of(b, span), h].astype(F32) * grads[:, None, :]
+            sums = jnp.sum(terms, axis=-1)
+            for k in range(2):
+                found = jnp.where(lane == 2 * h + k, sums[:, k : k + 1], found)
+        gates[rows_of(b, span), :] = found
+
+    turned = gates[...].T
+    for h in range(heads):
+        cols = pl.ds(h * tokens, tokens)
+        dg[:, cols] = jnp.where(slot[:, cols] >= 0, turned[2 * h : 2 * h + 2, :], 0.0)
+
+    for c in wloads:
+        c.wait()
+
+    others = [lax.rem(row + i, halves) for i in range(1, halves)]
+
+    def from_rows(m, n):
+        for t in others:
+            landed(held(m, 2 * t + side, n), wy_recv.at[m, n, t]).wait()
+            w_twin(m, n, t).start()
+
+    before = None
+    for m, n in pieces:
+        landed(held(m, mine, n), wz_recv.at[m, n]).wait()
+        w_twin(m, n, row).start()
+        for t in others:
+            w_row(m, n, t).start()
+        if before is not None:
+            from_rows(*before)
+        before = (m, n)
+
+    @pl.when(jnp.logical_not(outer))
+    def _():
+        for m, n in pieces:
+            w_cross(m, n).start()
+
+    from_rows(*before)
+    for m, n in pieces:
+        for t in range(halves):
+            landed(held(m, 2 * t + (1 - side), n), wt_recv.at[m, n, t]).wait()
+
+    def process(f, s, n):
+        for step in range(s, s + n):
+            if step > 0:
+                for v, dst in enumerate((rx, rg)):
+                    landed(dst.at[fixed(f, step)], xg_recv.at[v, f, step]).wait()
+        rows = fixed(f, s, n)
+        for c in range(ff // tile):
+            cols = pl.ds(c * tile, tile)
+            z = dot(rx[rows, :], win[f, :, cols], 1, 0)
+            e = dot(rg[rows, :], wout[f, cols, :], 1, 1)
+            zz = z * z
+            t = jnp.tanh(ROOT * (z + CUBE * (zz * z)))
+            part = 0.5 * (1.0 + t)
+            hb[rows, cols] = (z * part).astype(BF16)
+            slope = part + 0.5 * z * (1.0 - t * t) * (ROOT * (1.0 + 3.0 * CUBE * zz))
+            fb[rows, cols] = (e * slope).astype(BF16)
+        for c in range(sub // tile):
+            cols = pl.ds(c * tile, tile)
+            back = dot(fb[rows, :], win[f, cols, :], 1, 1).astype(BF16)
+            for step in range(s, s + n):
+                piece = back[(step - s) * cap : (step - s + 1) * cap]
+                if step == 0:
+                    rr[fixed(f, step), cols] = piece
+                else:
+                    rs[fixed(f, step), cols] = piece
+        for step in range(s, s + n):
+            if step > 0:
+                r_copy(f, step).start()
+
+    block = dwo.shape[1]
+
+    def product(f, q):
+        cols = rows_of(q, block)
+        rows = fixed(f, 0, half)
+        po[f, q] = dot(hb[rows, cols], rg[rows, :], 0, 0).astype(BF16)
+        pi[f, q] = dot(rx[rows, cols], fb[rows, :], 0, 0).astype(BF16)
+
+    def exchange(f):
+        @pl.loop(0, halves)
+        def _(i):
+            t = lax.rem(row + 1 + i, halves)
+            product(f, 2 * t + (1 - side))
+            twin_copy(f, 0, 2 * t + (1 - side), t).start()
+            twin_copy(f, 1, 2 * t + (1 - side), t).start()
+            product(f, 2 * t + side)
+
+            @pl.when(t != row)
+            def _():
+                for s, (own, got, out) in enumerate(((po, tpo, so), (pi, tpi, si))):
+                    landed(got.at[f, t], t_recv.at[f, s, t]).wait()
+                    out[f, t] = (own[f, 2 * t + side].astype(F32) + got[f, t].astype(F32)).astype(BF16)
+                    row_copy(f, s, t).start()
+
+    def total(f, s):
+        own, got, sums = ((po, tpo, rpo), (pi, tpi, rpi))[s]
+        landed(got.at[f, row], t_recv.at[f, s, row]).wait()
+        out = own[f, mine].astype(F32) + got[f, row].astype(F32)
+        for t in others:
+            row_got(f, s, t).wait()
+            out = out + sums[f, t].astype(F32)
+        return out
+
+    def scatter(f, s, n, start=False):
+        ones = []
+        for step in range(s, s + n):
+            if step > 0:
+                landed(rr.at[fixed(f, step)], r_recv.at[f, step]).wait()
+            h0, h1 = hot(f, step)
+            ones.append((h0 | h1).astype(F32).astype(BF16))
+        more = dot(jnp.concatenate(ones, axis=0), rr[fixed(f, s, n), :], 0, 0)
+        acc[...] = more if start else acc[...] + more
+
+    process(1, 0, half // 2)
+    process(1, half // 2, half // 2)
+    exchange(1)
+
+    @pl.when(jnp.logical_not(outer))
+    def _():
+        for step in far_steps:
+            xg_copy(0, 0, step).start()
+            xg_copy(1, 0, step).start()
+
+    process(0, 0, half // 2)
+    for s, out in enumerate((cpo, cpi)):
+        out[...] = total(1, s).astype(BF16)
+        cross_copy(s).start()
+    process(0, half // 2, half // 2)
+    exchange(0)
+    scatter(1, 0, half // 2, True)
+    scatter(1, half // 2, half // 2)
+    for s, out in enumerate((dwo, dwi)):
+        out[0] = total(0, s)
+    scatter(0, 0, half // 2)
+    scatter(0, half // 2, half // 2)
+    for h in range(heads):
+        dx[:, pl.ds(h * sub, sub)] = acc[pl.ds(h * tokens, tokens), :].astype(BF16)
+    for s, (out, got) in enumerate(((dwo, gpo), (dwi, gpi))):
+        landed(got, c_recv.at[s]).wait()
+        out[0] = out[0] + got[...].astype(F32)
+
+    for f in range(2):
+        for step in near:
+            xg_copy(0, f, step).wait_send()
+            xg_copy(1, f, step).wait_send()
+            r_copy(f, step).wait_send()
+        for s in range(2):
+            for t in range(halves):
+                twin_copy(f, s, 2 * t + (1 - side), t).wait_send()
+            for t in others:
+                row_copy(f, s, t).wait_send()
+    for m, n in pieces:
+        w_cross(m, n).wait_send()
+        for t in range(halves):
+            w_twin(m, n, t).wait_send()
+        for t in others:
+            w_row(m, n, t).wait_send()
+    for s in range(2):
+        cross_copy(s).wait_send()
+
+
+def paired_call(
+    sub_inputs,
+    out_grads,
+    expert_outputs,
+    combine_weights,
+    expert_ids,
+    slot_ids,
+    expert_input_weight,
+    expert_output_weight,
+):
+    tokens, heads, top = expert_ids.shape
+    _, sub, ff = expert_input_weight.shape
+    groups = lax.axis_size("expert")
+    replicas = lax.axis_size("dp")
+    cap = top * heads * tokens // groups
+
+    def flat(a):
+        return a.transpose(2, 1, 0).reshape(top, heads * tokens)
+
+    slots = groups * cap
+    half = groups // 2
+    halves = replicas // 2
+    part = sub // replicas
+    part_out = ff // replicas
+    dims = (groups, replicas, cap, heads, tokens, sub, ff)
+    any_spec = pl.BlockSpec(memory_space=pltpu.HBM)
+    vmem = pl.BlockSpec(memory_space=pltpu.VMEM)
+    dma = pltpu.SemaphoreType.DMA
+    rows = heads * tokens
+    d_inputs, dw_in, dw_out, gate_dots = pl.pallas_call(
+        functools.partial(paired, dims),
+        out_shape=(
+            jax.ShapeDtypeStruct((tokens, heads * sub), BF16),
+            jax.ShapeDtypeStruct((1, part, ff), F32),
+            jax.ShapeDtypeStruct((1, part_out, sub), F32),
+            jax.ShapeDtypeStruct((top, heads * tokens), F32),
+        ),
+        in_specs=[vmem, vmem, vmem, any_spec, any_spec, any_spec, any_spec, any_spec],
+        out_specs=(vmem, vmem, vmem, vmem),
+        scratch_shapes=[
+            pltpu.VMEM((top, rows), jnp.int32),
+            pltpu.VMEM((rows, sub), BF16),
+            pltpu.VMEM((rows, sub), BF16),
+            pltpu.VMEM((2, sub, ff), BF16),
+            pltpu.VMEM((2, ff, sub), BF16),
+            *[pltpu.VMEM((slots, sub), BF16)] * 6,
+            pltpu.VMEM((slots, ff), BF16),
+            pltpu.VMEM((slots, ff), BF16),
+            pltpu.VMEM((rows, sub), F32),
+            pltpu.VMEM((2, replicas, part_out, sub), BF16),
+            pltpu.VMEM((2, replicas, part, ff), BF16),
+            *[pltpu.VMEM((2, halves, part_out, sub), BF16), pltpu.VMEM((2, halves, part, ff), BF16)] * 3,
+            *[pltpu.VMEM((part_out, sub), BF16), pltpu.VMEM((part, ff), BF16)] * 2,
+            pltpu.VMEM((tokens, heads, top, sub), BF16),
+            pltpu.VMEM((tokens, 128), F32),
+            dma((2 * heads + 3,)),
+            *[dma((2, 2, half))] * 2,
+            *[dma((2, half))] * 2,
+            *[dma((2, PIECES))] * 2,
+            *[dma((2, PIECES, halves))] * 4,
+            *[dma((2, 2, halves))] * 4,
+            *[dma((2,))] * 2,
+        ],
+        compiler_params=pltpu.CompilerParams(
+            collective_id=0, has_side_effects=True, vmem_limit_bytes=63 * 1024 * 1024
+        ),
+        cost_estimate=pl.CostEstimate(flops=20 * 10**9, bytes_accessed=2**24, transcendentals=0),
+    )(
+        flat(expert_ids), flat(slot_ids), flat(combine_weights),
+        sub_inputs, out_grads, expert_input_weight, expert_output_weight, expert_outputs,
+    )
+    d_gates = gate_dots.reshape(top, heads, tokens).transpose(2, 1, 0)
+    return (d_inputs, d_gates, dw_in, dw_out)
+
+
+def on_device(*args):
+    tokens, heads, top = args[4].shape
+    _, sub, ff = args[6].shape
+    groups = lax.axis_size("expert")
+    replicas = lax.axis_size("dp")
+    cap = top * heads * tokens // groups
+    half = groups // 2
+    fits = half >= 4 and half & (half - 1) == 0 and replicas % 2 == 0 and cap % 128 == 0 and tokens % 128 == 0
+    tokens_cross = half * replicas * cap * 3 * sub
+    weights_cross = 4 * sub * ff
+    if fits and weights_cross < tokens_cross:
+        return paired_call(*args)
+    return plain_call(*args)
+
+
 def solution(mesh):
     rows = P(("expert", "dp"), None)
     table = P(("expert", "dp"), None, None)

time: 164 us -> 145 us (0.88)
  the two profiles are of different devices: /device:TPU:9 before, /device:TPU:0 now
where the time goes in v1:
time: 145 us; the launch traced here: 144 us
  Pallas kernels  139 us (96%)
  local copies, waits for them, and re-layouts  4.98 us (3%)
    pallas_call x1, Pallas kernels, paired_call(): pl.pallas_call(functools.partial(paired, dims), out_shape=(jax.ShapeDtype...  139 us
    unnamed x10, local copies, waits for them, and re-layouts  4.98 us

profile of v1, /device:TPU:0, one launch (start us, length us, event | category | flops | bytes accessed | tf_op | source)
XLA Modules:
  0.0 144.3 jit_solution(12808441083475143859)
XLA Ops:
  0.6 138.7 %shard_map.111 = (bf16[128,4096]{1,0:T(8,128)(2,1)}, f32[1,256,1024]{2,1,0:T(8,128)}, f32[1,256,1024]{2,1,0:T(8,128)}, f32[2,512]{1,0:T(2,128)}) custom-call(s32[2,512]{1,0:T(2,128)} %bitcast.13, s32[2,512]{1,0:T(2,128)} %bitcast.14, f32[2,512]{1,0:T(2,128)} %bitcast.15, bf16[128,4096]{1,0:T(8,128)(2,1)} %x_hbm.1, bf16[128,4096]{1,0:T(8,128)(2,1)} %g_hbm.1, ...), custom_call_target="tpu_custom_call" | custom-call | flops 20000000000 | bytes 16777216 | tf_op jit(solution)/shard_map/pallas_call | solution.py:701
  139.3 0.0 copy-start.2
  139.3 0.0 copy-start.1
  139.3 0.0 copy-start
  139.3 2.4 %copy.17 = bf16[128,4096]{1,0:T(8,128)(2,1)} copy(bf16[128,4096]{1,0:T(8,128)(2,1)} %get-tuple-element.16) | data formatting | bytes 2097152
  141.8 0.0 copy-done.2
  141.8 0.6 copy.18
  142.4 0.0 copy-done.1
  142.4 1.0 copy.19
  143.3 0.0 copy-done
  143.4 1.0 copy.20
Async XLA Ops:
  139.3 2.5 %copy-start.2 = (f32[2,512]{1,0:T(2,128)S(1)}, f32[2,512]{1,0:T(2,128)}, u32[]{:S(2)}) copy-start(f32[2,512]{1,0:T(2,128)} %get-tuple-element.9) | copy-start | bytes 12292
  139.3 3.1 %copy-start.1 = (f32[1,256,1024]{2,1,0:T(8,128)S(1)}, f32[1,256,1024]{2,1,0:T(8,128)}, u32[]{:S(2)}) copy-start(f32[1,256,1024]{2,1,0:T(8,128)} %get-tuple-element.18) | copy-start | bytes 3145732
  139.3 4.0 %copy-start = (f32[1,256,1024]{2,1,0:T(8,128)S(1)}, f32[1,256,1024]{2,1,0:T(8,128)}, u32[]{:S(2)}) copy-start(f32[1,256,1024]{2,1,0:T(8,128)} %get-tuple-element.19) | copy-start | bytes 3145732

commit v2 on v1

--- a/solution.py
+++ b/solution.py
@@ -352,7 +352,9 @@
     low = lax.rem(me, half)
     base = me - low
     opposite = lax.rem(me + half, groups)
-    outer = me // half == low // (half // 2)
+    inner = lax.rem(me // half + low // (half // 2), 2)
+    outer = inner == 0
+    first, second = inner, 1 - inner
     row, side = mine // 2, mine % 2
     twin = row * 2 + (1 - side)
     near = range(1, half)
@@ -361,7 +363,7 @@
         return pl.ds(pl.multiple_of(index * size, size), size)
 
     def fixed(f, s, n=1):
-        return pl.ds((f * half + s) * cap, n * cap)
+        return pl.ds(pl.multiple_of((f * half + s) * cap, cap), n * cap)
 
     def landed(ref, sem):
         return pltpu.make_async_copy(ref, ref, sem)
@@ -477,27 +479,30 @@
     for c in loads:
         c.wait()
     far_steps = range(half // 2, half)
-    near_steps = range(1, half // 2)
-
-    for f in (1, 0):
-
-        @pl.loop(0, half - 1)
-        def _(i):
-            step = lax.rem(i + half // 2 - 1, half - 1) + 1
-            gather(f, step, sx, sg)
-            if f == 1:
-                xg_copy(0, f, step).start()
-                xg_copy(1, f, step).start()
-            else:
-
-                @pl.when(jnp.logical_or(outer, step < half // 2))
-                def _():
-                    xg_copy(0, f, step).start()
-                    xg_copy(1, f, step).start()
+
+    def send(f, step):
+        xg_copy(0, f, step).start()
+        xg_copy(1, f, step).start()
 
     @pl.loop(0, 2)
-    def _(f):
-        gather(f, 0, rx, rg)
+    def _(i):
+        f_far = second + i * (first - second)
+        f_near = first + i * (second - first)
+
+        @pl.loop(half // 2, half)
+        def _(step):
+            gather(f_far, step, sx, sg)
+
+            @pl.when(jnp.logical_or(outer, i == 0))
+            def _():
+                send(f_far, step)
+
+        @pl.loop(1, half // 2)
+        def _(step):
+            gather(f_near, step, sx, sg)
+            send(f_near, step)
+
+        gather(f_near, 0, rx, rg)
 
     eload.wait()
     span = 16
@@ -529,31 +534,34 @@
             landed(held(m, 2 * t + side, n), wy_recv.at[m, n, t]).wait()
             w_twin(m, n, t).start()
 
-    before = None
-    for m, n in pieces:
-        landed(held(m, mine, n), wz_recv.at[m, n]).wait()
-        w_twin(m, n, row).start()
-        for t in others:
-            w_row(m, n, t).start()
-        if before is not None:
-            from_rows(*before)
-        before = (m, n)
-
-    @pl.when(jnp.logical_not(outer))
-    def _():
+    def weights():
+        before = None
         for m, n in pieces:
-            w_cross(m, n).start()
-
-    from_rows(*before)
-    for m, n in pieces:
-        for t in range(halves):
-            landed(held(m, 2 * t + (1 - side), n), wt_recv.at[m, n, t]).wait()
-
-    def process(f, s, n):
+            landed(held(m, mine, n), wz_recv.at[m, n]).wait()
+            w_twin(m, n, row).start()
+            for t in others:
+                w_row(m, n, t).start()
+            if before is not None:
+                from_rows(*before)
+            before = (m, n)
+
+        @pl.when(jnp.logical_not(outer))
+        def _():
+            for m, n in pieces:
+                w_cross(m, n).start()
+
+        from_rows(*before)
+        for m, n in pieces:
+            for t in range(halves):
+                landed(held(m, 2 * t + (1 - side), n), wt_recv.at[m, n, t]).wait()
+
+    def arrive(f, s, n):
         for step in range(s, s + n):
             if step > 0:
                 for v, dst in enumerate((rx, rg)):
                     landed(dst.at[fixed(f, step)], xg_recv.at[v, f, step]).wait()
+
+    def process(f, s, n):
         rows = fixed(f, s, n)
         for c in range(ff // tile):
             cols = pl.ds(c * tile, tile)
@@ -574,6 +582,8 @@
                     rr[fixed(f, step), cols] = piece
                 else:
                     rs[fixed(f, step), cols] = piece
+
+    def reply(f, s, n):
         for step in range(s, s + n):
             if step > 0:
                 r_copy(f, step).start()
@@ -586,7 +596,7 @@
         po[f, q] = dot(hb[rows, cols], rg[rows, :], 0, 0).astype(BF16)
         pi[f, q] = dot(rx[rows, cols], fb[rows, :], 0, 0).astype(BF16)
 
-    def exchange(f):
+    def exchange(f, early):
         @pl.loop(0, halves)
         def _(i):
             t = lax.rem(row + 1 + i, halves)
@@ -600,7 +610,10 @@
                 for s, (own, got, out) in enumerate(((po, tpo, so), (pi, tpi, si))):
                     landed(got.at[f, t], t_recv.at[f, s, t]).wait()
                     out[f, t] = (own[f, 2 * t + side].astype(F32) + got[f, t].astype(F32)).astype(BF16)
-                    row_copy(f, s, t).start()
+                    if s == 0 or not early:
+                        row_copy(f, s, t).start()
+                    else:
+                        pl.when(inner == 1)(lambda s=s: row_copy(f, s, t).start())
 
     def total(f, s):
         own, got, sums = ((po, tpo, rpo), (pi, tpi, rpi))[s]
@@ -621,38 +634,72 @@
         more = dot(jnp.concatenate(ones, axis=0), rr[fixed(f, s, n), :], 0, 0)
         acc[...] = more if start else acc[...] + more
 
-    process(1, 0, half // 2)
-    process(1, half // 2, half // 2)
-    exchange(1)
-
-    @pl.when(jnp.logical_not(outer))
+    def pass_on(s):
+        out = (cpo, cpi)[s]
+        out[...] = total(1, s).astype(BF16)
+        cross_copy(s).start()
+
+    near_part, far_part = (0, half // 2), (half // 2, half // 2)
+    pl.when(inner == 1)(weights)
+    arrive(first, *near_part)
+    process(first, *near_part)
+    reply(first, *near_part)
+    arrive(first, *far_part)
+
+    @pl.when(inner == 1)
     def _():
         for step in far_steps:
-            xg_copy(0, 0, step).start()
-            xg_copy(1, 0, step).start()
-
-    process(0, 0, half // 2)
-    for s, out in enumerate((cpo, cpi)):
-        out[...] = total(1, s).astype(BF16)
-        cross_copy(s).start()
-    process(0, half // 2, half // 2)
-    exchange(0)
-    scatter(1, 0, half // 2, True)
-    scatter(1, half // 2, half // 2)
+            send(first, step)
+
+    process(first, *far_part)
+    pl.when(outer)(lambda: reply(first, *far_part))
+    exchange(first, True)
+    pl.when(outer)(weights)
+    arrive(second, *near_part)
+    process(second, *near_part)
+    reply(second, *near_part)
+    arrive(second, *far_part)
+    for step in far_steps:
+        xg_copy(0, first, step).wait_send()
+        xg_copy(1, first, step).wait_send()
+    pl.when(inner == 1)(lambda: reply(first, *far_part))
+    process(second, *far_part)
+    reply(second, *far_part)
+
+    @pl.when(inner == 1)
+    def _():
+        pass_on(0)
+        pass_on(1)
+
+    exchange(second, False)
+
+    @pl.when(outer)
+    def _():
+        for t in others:
+            row_copy(first, 1, t).start()
+        pass_on(0)
+        pass_on(1)
+
+    scatter(first, 0, half // 2, True)
+    scatter(second, 0, half // 2)
+    scatter(second, half // 2, half // 2)
     for s, out in enumerate((dwo, dwi)):
         out[0] = total(0, s)
-    scatter(0, 0, half // 2)
-    scatter(0, half // 2, half // 2)
+    scatter(first, half // 2, half // 2)
     for h in range(heads):
         dx[:, pl.ds(h * sub, sub)] = acc[pl.ds(h * tokens, tokens), :].astype(BF16)
     for s, (out, got) in enumerate(((dwo, gpo), (dwi, gpi))):
         landed(got, c_recv.at[s]).wait()
         out[0] = out[0] + got[...].astype(F32)
 
+    for step in far_steps:
+        xg_copy(0, second, step).wait_send()
+        xg_copy(1, second, step).wait_send()
     for f in range(2):
         for step in near:
-            xg_copy(0, f, step).wait_send()
-            xg_copy(1, f, step).wait_send()
+            if step < half // 2:
+                xg_copy(0, f, step).wait_send()
+                xg_copy(1, f, step).wait_send()
             r_copy(f, step).wait_send()
         for s in range(2):
             for t in range(halves):

time: 145 us -> 135 us (0.931)
  Pallas kernels: 139 us -> 129 us
    pallas_call x1, Pallas kernels: 139 us -> 129 us  [paired_call(): pl.pallas_call(functools.partial(paired, dims), out_shape=(jax.ShapeDtype...]
where the time goes in v2:
time: 135 us; the launch traced here: 134 us
  Pallas kernels  129 us (96%)
  local copies, waits for them, and re-layouts  4.98 us (4%)
    pallas_call x1, Pallas kernels, paired_call(): pl.pallas_call(functools.partial(paired, dims), out_shape=(jax.ShapeDtype...  129 us
    unnamed x10, local copies, waits for them, and re-layouts  4.98 us

profile of v2, /device:TPU:0, one launch (start us, length us, event | category | flops | bytes accessed | tf_op | source)
XLA Modules:
  0.0 134.3 jit_solution(15695069259910391758)
XLA Ops:
  0.6 128.7 %shard_map.111 = (bf16[128,4096]{1,0:T(8,128)(2,1)}, f32[1,256,1024]{2,1,0:T(8,128)}, f32[1,256,1024]{2,1,0:T(8,128)}, f32[2,512]{1,0:T(2,128)}) custom-call(s32[2,512]{1,0:T(2,128)} %bitcast.13, s32[2,512]{1,0:T(2,128)} %bitcast.14, f32[2,512]{1,0:T(2,128)} %bitcast.15, bf16[128,4096]{1,0:T(8,128)(2,1)} %x_hbm.1, bf16[128,4096]{1,0:T(8,128)(2,1)} %g_hbm.1, ...), custom_call_target="tpu_custom_call" | custom-call | flops 20000000000 | bytes 16777216 | tf_op jit(solution)/shard_map/pallas_call | solution.py:748
  129.3 0.0 copy-start.2
  129.3 0.0 copy-start.1
  129.4 0.0 copy-start
  129.4 2.4 %copy.17 = bf16[128,4096]{1,0:T(8,128)(2,1)} copy(bf16[128,4096]{1,0:T(8,128)(2,1)} %get-tuple-element.16) | data formatting | bytes 2097152
  131.8 0.0 copy-done.2
  131.8 0.6 copy.18
  132.4 0.0 copy-done.1
  132.4 1.0 copy.19
  133.4 0.0 copy-done
  133.4 1.0 copy.20
Async XLA Ops:
  129.3 2.5 %copy-start.2 = (f32[2,512]{1,0:T(2,128)S(1)}, f32[2,512]{1,0:T(2,128)}, u32[]{:S(2)}) copy-start(f32[2,512]{1,0:T(2,128)} %get-tuple-element.9) | copy-start | bytes 12292
  129.3 3.1 %copy-start.1 = (f32[1,256,1024]{2,1,0:T(8,128)S(1)}, f32[1,256,1024]{2,1,0:T(8,128)}, u32[]{:S(2)}) copy-start(f32[1,256,1024]{2,1,0:T(8,128)} %get-tuple-element.18) | copy-start | bytes 3145732
  129.4 4.0 %copy-start = (f32[1,256,1024]{2,1,0:T(8,128)S(1)}, f32[1,256,1024]{2,1,0:T(8,128)}, u32[]{:S(2)}) copy-start(f32[1,256,1024]{2,1,0:T(8,128)} %get-tuple-element.19) | copy-start | bytes 3145732

commit v3 on v2

--- a/solution.py
+++ b/solution.py
@@ -397,8 +397,6 @@
     pl.semaphore_signal(barrier, inc=1, device_id={"expert": opposite}, device_id_type=MESH)
     for i in range(1, replicas):
         pl.semaphore_signal(barrier, inc=1, device_id={"dp": lax.rem(mine + i, replicas)}, device_id_type=MESH)
-    pl.semaphore_wait(barrier, half + replicas - 1)
-
     def owner(s):
         return base + partner(low, s, half)
 
@@ -440,26 +438,24 @@
         src, dst = ((po, tpo), (pi, tpi))[s]
         return remote(src.at[f, q], dst.at[f, t], t_send.at[f, s, t], t_recv.at[f, s, t], {"dp": twin})
 
-    def row_copy(f, s, t):
+    def cut(s, n):
+        size = (dwo, dwi)[s].shape[1] // PIECES
+        return pl.ds(n * size, size)
+
+    def row_copy(f, s, t, n):
         src, dst = ((so, rpo), (si, rpi))[s]
         return remote(
-            src.at[f, t], dst.at[f, row], y_send.at[f, s, t], y_recv.at[f, s, row], {"dp": 2 * t + side}
-        )
-
-    def row_got(f, s, t):
-        ref = (rpo, rpi)[s].at[f, t]
-        return landed(ref, y_recv.at[f, s, t])
-
-    def cross_copy(s):
+            src.at[f, t, cut(s, n)], dst.at[f, row, cut(s, n)],
+            y_send.at[f, s, n, t], y_recv.at[f, s, n, row], {"dp": 2 * t + side},
+        )
+
+    def cross_copy(s, n):
         src, dst = ((cpo, gpo), (cpi, gpi))[s]
-        return remote(src, dst, c_send.at[s], c_recv.at[s], {"expert": opposite})
+        return remote(
+            src.at[cut(s, n)], dst.at[cut(s, n)], c_send.at[s, n], c_recv.at[s, n], {"expert": opposite}
+        )
 
     pieces = [(m, n) for m in range(2) for n in range(PIECES)]
-
-    @pl.when(outer)
-    def _():
-        for m, n in pieces:
-            w_cross(m, n).start()
 
     tgt[...] = jnp.where(slot[...] >= 0, ids[...] * cap + slot[...], -1)
 
@@ -484,25 +480,35 @@
         xg_copy(0, f, step).start()
         xg_copy(1, f, step).start()
 
+    @pl.loop(half // 2, half)
+    def _(step):
+        gather(second, step, sx, sg)
+
+    pl.semaphore_wait(barrier, half + replicas - 1)
+
+    @pl.when(outer)
+    def _():
+        for m, n in pieces:
+            w_cross(m, n).start()
+
+    for step in far_steps:
+        send(second, step)
+
     @pl.loop(0, 2)
     def _(i):
-        f_far = second + i * (first - second)
-        f_near = first + i * (second - first)
-
-        @pl.loop(half // 2, half)
-        def _(step):
-            gather(f_far, step, sx, sg)
-
-            @pl.when(jnp.logical_or(outer, i == 0))
-            def _():
-                send(f_far, step)
+        f = first + i * (second - first)
 
         @pl.loop(1, half // 2)
         def _(step):
-            gather(f_near, step, sx, sg)
-            send(f_near, step)
-
-        gather(f_near, 0, rx, rg)
+            gather(f, step, sx, sg)
+            send(f, step)
+
+        gather(f, 0, rx, rg)
+
+    @pl.loop(half // 2, half)
+    def _(step):
+        gather(first, step, sx, sg)
+        pl.when(outer)(lambda: send(first, step))
 
     eload.wait()
     span = 16
@@ -544,11 +550,13 @@
             if before is not None:
                 from_rows(*before)
             before = (m, n)
-
-        @pl.when(jnp.logical_not(outer))
-        def _():
-            for m, n in pieces:
-                w_cross(m, n).start()
+            if before == pieces[-1]:
+
+                @pl.when(inner == 1)
+                def _():
+                    xg_copy(0, first, half // 2).start()
+                    for piece in pieces:
+                        w_cross(*piece).start()
 
         from_rows(*before)
         for m, n in pieces:
@@ -596,6 +604,10 @@
         po[f, q] = dot(hb[rows, cols], rg[rows, :], 0, 0).astype(BF16)
         pi[f, q] = dot(rx[rows, cols], fb[rows, :], 0, 0).astype(BF16)
 
+    def rows_out(f, s, t):
+        for n in range(PIECES):
+            row_copy(f, s, t, n).start()
+
     def exchange(f, early):
         @pl.loop(0, halves)
         def _(i):
@@ -611,17 +623,18 @@
                     landed(got.at[f, t], t_recv.at[f, s, t]).wait()
                     out[f, t] = (own[f, 2 * t + side].astype(F32) + got[f, t].astype(F32)).astype(BF16)
                     if s == 0 or not early:
-                        row_copy(f, s, t).start()
+                        rows_out(f, s, t)
                     else:
-                        pl.when(inner == 1)(lambda s=s: row_copy(f, s, t).start())
-
-    def total(f, s):
+                        pl.when(inner == 1)(lambda s=s: rows_out(f, s, t))
+
+    def total(f, s, n):
         own, got, sums = ((po, tpo, rpo), (pi, tpi, rpi))[s]
-        landed(got.at[f, row], t_recv.at[f, s, row]).wait()
-        out = own[f, mine].astype(F32) + got[f, row].astype(F32)
+        if n == 0:
+            landed(got.at[f, row], t_recv.at[f, s, row]).wait()
+        out = own[f, mine, cut(s, n)].astype(F32) + got[f, row, cut(s, n)].astype(F32)
         for t in others:
-            row_got(f, s, t).wait()
-            out = out + sums[f, t].astype(F32)
+            landed(sums.at[f, t, cut(s, n)], y_recv.at[f, s, n, t]).wait()
+            out = out + sums[f, t, cut(s, n)].astype(F32)
         return out
 
     def scatter(f, s, n, start=False):
@@ -636,8 +649,9 @@
 
     def pass_on(s):
         out = (cpo, cpi)[s]
-        out[...] = total(1, s).astype(BF16)
-        cross_copy(s).start()
+        for n in range(PIECES):
+            out[cut(s, n)] = total(1, s, n).astype(BF16)
+            cross_copy(s, n).start()
 
     near_part, far_part = (0, half // 2), (half // 2, half // 2)
     pl.when(inner == 1)(weights)
@@ -648,7 +662,8 @@
 
     @pl.when(inner == 1)
     def _():
-        for step in far_steps:
+        xg_copy(1, first, half // 2).start()
+        for step in far_steps[1:]:
             send(first, step)
 
     process(first, *far_part)
@@ -676,7 +691,7 @@
     @pl.when(outer)
     def _():
         for t in others:
-            row_copy(first, 1, t).start()
+            rows_out(first, 1, t)
         pass_on(0)
         pass_on(1)
 
@@ -684,13 +699,15 @@
     scatter(second, 0, half // 2)
     scatter(second, half // 2, half // 2)
     for s, out in enumerate((dwo, dwi)):
-        out[0] = total(0, s)
+        for n in range(PIECES):
+            out[0, cut(s, n)] = total(0, s, n)
     scatter(first, half // 2, half // 2)
     for h in range(heads):
         dx[:, pl.ds(h * sub, sub)] = acc[pl.ds(h * tokens, tokens), :].astype(BF16)
     for s, (out, got) in enumerate(((dwo, gpo), (dwi, gpi))):
-        landed(got, c_recv.at[s]).wait()
-        out[0] = out[0] + got[...].astype(F32)
+        for n in range(PIECES):
+            landed(got.at[cut(s, n)], c_recv.at[s, n]).wait()
+            out[0, cut(s, n)] = out[0, cut(s, n)] + got[cut(s, n)].astype(F32)
 
     for step in far_steps:
         xg_copy(0, second, step).wait_send()
@@ -705,7 +722,8 @@
             for t in range(halves):
                 twin_copy(f, s, 2 * t + (1 - side), t).wait_send()
             for t in others:
-                row_copy(f, s, t).wait_send()
+                for n in range(PIECES):
+                    row_copy(f, s, t, n).wait_send()
     for m, n in pieces:
         w_cross(m, n).wait_send()
         for t in range(halves):
@@ -713,7 +731,18 @@
         for t in others:
             w_row(m, n, t).wait_send()
     for s in range(2):
-        cross_copy(s).wait_send()
+        for n in range(PIECES):
+            cross_copy(s, n).wait_send()
+
+
+def put_out(*refs):
+    count = len(refs) // 2
+    sems = refs[-1]
+    copies = [pltpu.make_async_copy(refs[i], refs[count + i], sems.at[i]) for i in range(count)]
+    for c in copies:
+        c.start()
+    for c in copies:
+        c.wait()
 
 
 def paired_call(
@@ -745,14 +774,15 @@
     vmem = pl.BlockSpec(memory_space=pltpu.VMEM)
     dma = pltpu.SemaphoreType.DMA
     rows = heads * tokens
-    d_inputs, dw_in, dw_out, gate_dots = pl.pallas_call(
+    shapes = (
+        ((tokens, heads * sub), BF16),
+        ((1, part, ff), F32),
+        ((1, part_out, sub), F32),
+        ((top, heads * tokens), F32),
+    )
+    results = pl.pallas_call(
         functools.partial(paired, dims),
-        out_shape=(
-            jax.ShapeDtypeStruct((tokens, heads * sub), BF16),
-            jax.ShapeDtypeStruct((1, part, ff), F32),
-            jax.ShapeDtypeStruct((1, part_out, sub), F32),
-            jax.ShapeDtypeStruct((top, heads * tokens), F32),
-        ),
+        out_shape=tuple(pltpu.VMEM(shape, kind) for shape, kind in shapes),
         in_specs=[vmem, vmem, vmem, any_spec, any_spec, any_spec, any_spec, any_spec],
         out_specs=(vmem, vmem, vmem, vmem),
         scratch_shapes=[
@@ -776,17 +806,26 @@
             *[dma((2, half))] * 2,
             *[dma((2, PIECES))] * 2,
             *[dma((2, PIECES, halves))] * 4,
-            *[dma((2, 2, halves))] * 4,
-            *[dma((2,))] * 2,
+            *[dma((2, 2, halves))] * 2,
+            *[dma((2, 2, PIECES, halves))] * 2,
+            *[dma((2, PIECES))] * 2,
         ],
         compiler_params=pltpu.CompilerParams(
-            collective_id=0, has_side_effects=True, vmem_limit_bytes=63 * 1024 * 1024
+            collective_id=0, has_side_effects=True, vmem_limit_bytes=59 * 1024 * 1024
         ),
         cost_estimate=pl.CostEstimate(flops=20 * 10**9, bytes_accessed=2**24, transcendentals=0),
     )(
         flat(expert_ids), flat(slot_ids), flat(combine_weights),
         sub_inputs, out_grads, expert_input_weight, expert_output_weight, expert_outputs,
     )
+    d_inputs, dw_in, dw_out, gate_dots = pl.pallas_call(
+        put_out,
+        out_shape=tuple(jax.ShapeDtypeStruct(shape, kind) for shape, kind in shapes),
+        in_specs=[vmem] * len(shapes),
+        out_specs=(any_spec,) * len(shapes),
+        scratch_shapes=[dma((len(shapes),))],
+        compiler_params=pltpu.CompilerParams(vmem_limit_bytes=1024 * 1024),
+    )(*results)
     d_gates = gate_dots.reshape(top, heads, tokens).transpose(2, 1, 0)
     return (d_inputs, d_gates, dw_in, dw_out)
 

time: 135 us -> 130 us (0.963)
  local copies, waits for them, and re-layouts: 4.98 us -> 0 us
    unnamed x10 -> x0, local copies, waits for them, and re-layouts: 4.98 us -> none
    pallas_call x1 -> x2, Pallas kernels: 129 us -> 129 us  [the longest x1 127 us: paired_call(): pl.pallas_call(functools.partial(paired, dims), out_shape=tuple((pltpu.VM...]
where the time goes in v3:
time: 130 us
  Pallas kernels  129 us (99%)
    pallas_call x1, Pallas kernels, paired_call(): pl.pallas_call(functools.partial(paired, dims), out_shape=tuple((pltpu.VM...  127 us

profile of v3, /device:TPU:0, one launch (start us, length us, event | category | flops | bytes accessed | tf_op | source)
XLA Modules:
  0.0 129.7 jit_solution(4846554617118066348)
XLA Ops:
  0.6 127.2 %shard_map.111 = (bf16[128,4096]{1,0:T(8,128)(2,1)S(1)}, f32[1,256,1024]{2,1,0:T(8,128)S(1)}, f32[1,256,1024]{2,1,0:T(8,128)S(1)}, f32[2,512]{1,0:T(2,128)S(1)}) custom-call(s32[2,512]{1,0:T(2,128)} %bitcast.12, s32[2,512]{1,0:T(2,128)} %bitcast.13, f32[2,512]{1,0:T(2,128)} %bitcast.14, bf16[128,4096]{1,0:T(8,128)(2,1)} %x_hbm.1, bf16[128,4096]{1,0:T(8,128)(2,1)} %g_hbm.1, ...), custom_call_target="tpu_custom_call" | custom-call | flops 20000000000 | bytes 16777216 | tf_op jit(solution)/shard_map/pallas_call | solution.py:783
  127.8 1.7 %shard_map.112 = (bf16[128,4096]{1,0:T(8,128)(2,1)}, f32[1,256,1024]{2,1,0:T(8,128)}, f32[1,256,1024]{2,1,0:T(8,128)}, f32[2,512]{1,0:T(2,128)}) custom-call(bf16[128,4096]{1,0:T(8,128)(2,1)S(1)} %get-tuple-element.12.refs_0_, f32[1,256,1024]{2,1,0:T(8,128)S(1)} %get-tuple-element.13.refs_1_, f32[1,256,1024]{2,1,0:T(8,128)S(1)} %get-tuple-element.14.refs_2_, ...), custom_call_target="tpu_custom_call" | custom-call | tf_op jit(solution)/shard_map/pallas_call | solution.py:821

commit v4 on v3

--- a/solution.py
+++ b/solution.py
@@ -341,7 +341,7 @@
     tgt, xs, gs, win, wout, sx, sg, rx, rg, rs, rr, hb, fb, acc, po, pi, tpo, tpi, so, si, rpo, rpi,
     cpo, cpi, gpo, gpi, ev, gates,
     load_sem, xg_send, xg_recv, r_send, r_recv, wz_send, wz_recv, wt_send, wt_recv, wy_send, wy_recv,
-    t_send, t_recv, y_send, y_recv, c_send, c_recv,
+    t_send, t_recv, y_send, y_recv, c_send, c_recv, a_send, a_recv,
 ):
     groups, replicas, cap, heads, tokens, sub, ff = dims
     tile = 256
@@ -363,7 +363,7 @@
         return pl.ds(pl.multiple_of(index * size, size), size)
 
     def fixed(f, s, n=1):
-        return pl.ds(pl.multiple_of((f * half + s) * cap, cap), n * cap)
+        return pl.ds(pl.multiple_of((f * (half + 1) + s) * cap, cap), n * cap)
 
     def landed(ref, sem):
         return pltpu.make_async_copy(ref, ref, sem)
@@ -397,6 +397,12 @@
     pl.semaphore_signal(barrier, inc=1, device_id={"expert": opposite}, device_id_type=MESH)
     for i in range(1, replicas):
         pl.semaphore_signal(barrier, inc=1, device_id={"dp": lax.rem(mine + i, replicas)}, device_id_type=MESH)
+    turn = half // 2
+    across = lax.rem(base + partner(low, turn, half) + half, groups)
+
+    @pl.when(inner == 1)
+    def _():
+        pl.semaphore_signal(barrier, inc=1, device_id={"expert": across}, device_id_type=MESH)
     def owner(s):
         return base + partner(low, s, half)
 
@@ -428,6 +434,17 @@
             xg_send.at[s, f, step], xg_recv.at[s, f, step], {"expert": owner(step)},
         )
 
+    def across_copy(s):
+        src, dst = ((sx, rx), (sg, rg))[s]
+        return remote(
+            src.at[fixed(1, turn)], dst.at[fixed(0, half)], a_send.at[s], a_recv.at[s], {"expert": across}
+        )
+
+    def across_reply():
+        return remote(
+            rs.at[fixed(0, half)], rr.at[fixed(1, turn)], a_send.at[2], r_recv.at[1, turn], {"expert": across}
+        )
+
     def r_copy(f, step):
         return remote(
             rs.at[fixed(f, step)], rr.at[fixed(f, step)],
@@ -468,7 +485,7 @@
         h0, h1 = hot(f, step)
         one = (h0 | h1).astype(F32).astype(BF16)
         w = jnp.sum(jnp.where(h0, cw[0:1, :], 0.0) + jnp.where(h1, cw[1:2, :], 0.0), axis=1, keepdims=True)
-        rows = rows_of(f * half + step, cap)
+        rows = fixed(f, step)
         out_x[rows, :] = dot(one, xs[...], 1, 0).astype(BF16)
         out_g[rows, :] = (dot(one, gs[...], 1, 0) * w).astype(BF16)
 
@@ -484,7 +501,7 @@
     def _(step):
         gather(second, step, sx, sg)
 
-    pl.semaphore_wait(barrier, half + replicas - 1)
+    pl.semaphore_wait(barrier, half + replicas - 1 + inner)
 
     @pl.when(outer)
     def _():
@@ -539,6 +556,10 @@
         for t in others:
             landed(held(m, 2 * t + side, n), wy_recv.at[m, n, t]).wait()
             w_twin(m, n, t).start()
+
+    def rows_out(f, s, t):
+        for n in range(PIECES):
+            row_copy(f, s, t, n).start()
 
     def weights():
         before = None
@@ -552,9 +573,13 @@
             before = (m, n)
             if before == pieces[-1]:
 
+                @pl.when(outer)
+                def _():
+                    for t in others:
+                        rows_out(first, 0, t)
+
                 @pl.when(inner == 1)
                 def _():
-                    xg_copy(0, first, half // 2).start()
                     for piece in pieces:
                         w_cross(*piece).start()
 
@@ -568,6 +593,10 @@
             if step > 0:
                 for v, dst in enumerate((rx, rg)):
                     landed(dst.at[fixed(f, step)], xg_recv.at[v, f, step]).wait()
+
+    def arrive_across():
+        for v, dst in enumerate((rx, rg)):
+            landed(dst.at[fixed(0, half)], a_recv.at[v]).wait()
 
     def process(f, s, n):
         rows = fixed(f, s, n)
@@ -598,34 +627,30 @@
 
     block = dwo.shape[1]
 
-    def product(f, q):
+    def product(f, q, n):
         cols = rows_of(q, block)
-        rows = fixed(f, 0, half)
+        rows = fixed(f, 0, n)
         po[f, q] = dot(hb[rows, cols], rg[rows, :], 0, 0).astype(BF16)
         pi[f, q] = dot(rx[rows, cols], fb[rows, :], 0, 0).astype(BF16)
 
-    def rows_out(f, s, t):
-        for n in range(PIECES):
-            row_copy(f, s, t, n).start()
-
-    def exchange(f, early):
+    def exchange(f, early, n):
         @pl.loop(0, halves)
         def _(i):
             t = lax.rem(row + 1 + i, halves)
-            product(f, 2 * t + (1 - side))
+            product(f, 2 * t + (1 - side), n)
             twin_copy(f, 0, 2 * t + (1 - side), t).start()
             twin_copy(f, 1, 2 * t + (1 - side), t).start()
-            product(f, 2 * t + side)
+            product(f, 2 * t + side, n)
 
             @pl.when(t != row)
             def _():
                 for s, (own, got, out) in enumerate(((po, tpo, so), (pi, tpi, si))):
                     landed(got.at[f, t], t_recv.at[f, s, t]).wait()
                     out[f, t] = (own[f, 2 * t + side].astype(F32) + got[f, t].astype(F32)).astype(BF16)
-                    if s == 0 or not early:
+                    if early:
+                        pl.when(inner == 1)(lambda s=s: rows_out(f, s, t))
+                    else:
                         rows_out(f, s, t)
-                    else:
-                        pl.when(inner == 1)(lambda s=s: rows_out(f, s, t))
 
     def total(f, s, n):
         own, got, sums = ((po, tpo, rpo), (pi, tpi, rpi))[s]
@@ -653,7 +678,14 @@
             out[cut(s, n)] = total(1, s, n).astype(BF16)
             cross_copy(s, n).start()
 
-    near_part, far_part = (0, half // 2), (half // 2, half // 2)
+    near_part, far_part = (0, turn), (turn, turn)
+    last_part = (turn + 1, turn - 1)
+
+    @pl.when(outer)
+    def _():
+        rx[fixed(1, turn), :] = jnp.zeros((cap, sub), BF16)
+        rg[fixed(1, turn), :] = jnp.zeros((cap, sub), BF16)
+
     pl.when(inner == 1)(weights)
     arrive(first, *near_part)
     process(first, *near_part)
@@ -662,34 +694,44 @@
 
     @pl.when(inner == 1)
     def _():
-        xg_copy(1, first, half // 2).start()
         for step in far_steps[1:]:
             send(first, step)
+        across_copy(0).start()
+        across_copy(1).start()
 
     process(first, *far_part)
     pl.when(outer)(lambda: reply(first, *far_part))
-    exchange(first, True)
+    exchange(first, True, half)
     pl.when(outer)(weights)
     arrive(second, *near_part)
     process(second, *near_part)
     reply(second, *near_part)
-    arrive(second, *far_part)
-    for step in far_steps:
-        xg_copy(0, first, step).wait_send()
-        xg_copy(1, first, step).wait_send()
-    pl.when(inner == 1)(lambda: reply(first, *far_part))
-    process(second, *far_part)
-    reply(second, *far_part)
 
     @pl.when(inner == 1)
     def _():
+        for step in far_steps[1:]:
+            xg_copy(0, first, step).wait_send()
+            xg_copy(1, first, step).wait_send()
+        reply(first, *far_part)
+        arrive_across()
+        process(0, half, 1)
+        across_reply().start()
         pass_on(0)
+        arrive(second, turn, 1)
+
+    arrive(second, *last_part)
+    process(second, *far_part)
+    pl.when(inner == 1)(lambda: reply(second, turn, 1))
+    reply(second, *last_part)
+
+    @pl.when(inner == 1)
+    def _():
         pass_on(1)
-
-    exchange(second, False)
+        exchange(0, False, half + 1)
 
     @pl.when(outer)
     def _():
+        exchange(1, False, half)
         for t in others:
             rows_out(first, 1, t)
         pass_on(0)
@@ -712,12 +754,29 @@
     for step in far_steps:
         xg_copy(0, second, step).wait_send()
         xg_copy(1, second, step).wait_send()
+
+    @pl.when(outer)
+    def _():
+        for step in far_steps:
+            xg_copy(0, first, step).wait_send()
+            xg_copy(1, first, step).wait_send()
+        r_copy(first, turn).wait_send()
+
+    @pl.when(inner == 1)
+    def _():
+        across_copy(0).wait_send()
+        across_copy(1).wait_send()
+        across_reply().wait_send()
+        r_copy(first, turn).wait_send()
+        r_copy(second, turn).wait_send()
+
     for f in range(2):
         for step in near:
-            if step < half // 2:
+            if step < turn:
                 xg_copy(0, f, step).wait_send()
                 xg_copy(1, f, step).wait_send()
-            r_copy(f, step).wait_send()
+            if step != turn:
+                r_copy(f, step).wait_send()
         for s in range(2):
             for t in range(halves):
                 twin_copy(f, s, 2 * t + (1 - side), t).wait_send()
@@ -764,7 +823,7 @@
     def flat(a):
         return a.transpose(2, 1, 0).reshape(top, heads * tokens)
 
-    slots = groups * cap
+    slots = (groups + 1) * cap
     half = groups // 2
     halves = replicas // 2
     part = sub // replicas
@@ -809,6 +868,8 @@
             *[dma((2, 2, halves))] * 2,
             *[dma((2, 2, PIECES, halves))] * 2,
             *[dma((2, PIECES))] * 2,
+            dma((3,)),
+            dma((2,)),
         ],
         compiler_params=pltpu.CompilerParams(
             collective_id=0, has_side_effects=True, vmem_limit_bytes=59 * 1024 * 1024

time: 130 us -> 124 us (0.954)
  Pallas kernels: 129 us -> 123 us
    pallas_call x1, Pallas kernels: 127 us -> 121 us  [paired_call(): pl.pallas_call(functools.partial(paired, dims), out_shape=tuple((pltpu.VM...]
where the time goes in v4:
time: 124 us
  Pallas kernels  123 us (99%)
    pallas_call x1, Pallas kernels, paired_call(): pl.pallas_call(functools.partial(paired, dims), out_shape=tuple((pltpu.VM...  121 us

profile of v4, /device:TPU:0, one launch (start us, length us, event | category | flops | bytes accessed | tf_op | source)
XLA Modules:
  0.0 123.7 jit_solution(13391857109987477536)
XLA Ops:
  0.6 121.2 %shard_map.111 = (bf16[128,4096]{1,0:T(8,128)(2,1)S(1)}, f32[1,256,1024]{2,1,0:T(8,128)S(1)}, f32[1,256,1024]{2,1,0:T(8,128)S(1)}, f32[2,512]{1,0:T(2,128)S(1)}) custom-call(s32[2,512]{1,0:T(2,128)} %bitcast.12, s32[2,512]{1,0:T(2,128)} %bitcast.13, f32[2,512]{1,0:T(2,128)} %bitcast.14, bf16[128,4096]{1,0:T(8,128)(2,1)} %x_hbm.1, bf16[128,4096]{1,0:T(8,128)(2,1)} %g_hbm.1, ...), custom_call_target="tpu_custom_call" | custom-call | flops 20000000000 | bytes 16777216 | tf_op jit(solution)/shard_map/pallas_call | solution.py:842
  121.9 1.7 %shard_map.112 = (bf16[128,4096]{1,0:T(8,128)(2,1)}, f32[1,256,1024]{2,1,0:T(8,128)}, f32[1,256,1024]{2,1,0:T(8,128)}, f32[2,512]{1,0:T(2,128)}) custom-call(bf16[128,4096]{1,0:T(8,128)(2,1)S(1)} %get-tuple-element.12.refs_0_, f32[1,256,1024]{2,1,0:T(8,128)S(1)} %get-tuple-element.13.refs_1_, f32[1,256,1024]{2,1,0:T(8,128)S(1)} %get-tuple-element.14.refs_2_, ...), custom_call_target="tpu_custom_call" | custom-call | tf_op jit(solution)/shard_map/pallas_call | solution.py:882

commit v5 on v4

--- a/solution.py
+++ b/solution.py
@@ -336,9 +336,9 @@
 
 def paired(
     dims,
-    ids, slot, cw, x_hbm, g_hbm, win_hbm, wout_hbm, eo_hbm,
+    ids_hbm, slot_hbm, cw_hbm, x_hbm, g_hbm, win_hbm, wout_hbm, eo_hbm,
     dx, dwi, dwo, dg,
-    tgt, xs, gs, win, wout, sx, sg, rx, rg, rs, rr, hb, fb, acc, po, pi, tpo, tpi, so, si, rpo, rpi,
+    ids, slot, cw, tgt, xs, gs, win, wout, sx, sg, rx, rg, rs, rr, hb, fb, acc, po, pi, tpo, tpi, so, si, rpo, rpi,
     cpo, cpi, gpo, gpi, ev, gates,
     load_sem, xg_send, xg_recv, r_send, r_recv, wz_send, wz_recv, wt_send, wt_recv, wy_send, wy_recv,
     t_send, t_recv, y_send, y_recv, c_send, c_recv, a_send, a_recv,
@@ -386,9 +386,10 @@
         pltpu.make_async_copy(wout_hbm.at[0], wout.at[0], load_sem.at[2 * heads + 1]),
     ]
     eload = pltpu.make_async_copy(eo_hbm, ev, load_sem.at[2 * heads + 2])
-    for c in loads + wloads + [eload]:
-        c.start()
-
+    tables = [
+        pltpu.make_async_copy(src, dst, load_sem.at[2 * heads + 3 + i])
+        for i, (src, dst) in enumerate(((ids_hbm, ids), (slot_hbm, slot), (cw_hbm, cw)))
+    ]
     barrier = pltpu.get_barrier_semaphore()
     for s in near:
         pl.semaphore_signal(
@@ -403,6 +404,9 @@
     @pl.when(inner == 1)
     def _():
         pl.semaphore_signal(barrier, inc=1, device_id={"expert": across}, device_id_type=MESH)
+    for c in tables + loads + wloads + [eload]:
+        c.start()
+
     def owner(s):
         return base + partner(low, s, half)
 
@@ -474,6 +478,14 @@
 
     pieces = [(m, n) for m in range(2) for n in range(PIECES)]
 
+    @pl.when(outer)
+    def _():
+        pl.semaphore_wait(barrier, half + replicas - 1)
+        for m, n in pieces:
+            w_cross(m, n).start()
+
+    for c in tables:
+        c.wait()
     tgt[...] = jnp.where(slot[...] >= 0, ids[...] * cap + slot[...], -1)
 
     def hot(f, step):
@@ -501,12 +513,9 @@
     def _(step):
         gather(second, step, sx, sg)
 
-    pl.semaphore_wait(barrier, half + replicas - 1 + inner)
-
-    @pl.when(outer)
-    def _():
-        for m, n in pieces:
-            w_cross(m, n).start()
+    @pl.when(inner == 1)
+    def _():
+        pl.semaphore_wait(barrier, half + replicas)
 
     for step in far_steps:
         send(second, step)
@@ -557,8 +566,8 @@
             landed(held(m, 2 * t + side, n), wy_recv.at[m, n, t]).wait()
             w_twin(m, n, t).start()
 
-    def rows_out(f, s, t):
-        for n in range(PIECES):
+    def rows_out(f, s, t, parts=range(PIECES)):
+        for n in parts:
             row_copy(f, s, t, n).start()
 
     def weights():
@@ -672,9 +681,9 @@
         more = dot(jnp.concatenate(ones, axis=0), rr[fixed(f, s, n), :], 0, 0)
         acc[...] = more if start else acc[...] + more
 
-    def pass_on(s):
+    def pass_on(s, parts):
         out = (cpo, cpi)[s]
-        for n in range(PIECES):
+        for n in parts:
             out[cut(s, n)] = total(1, s, n).astype(BF16)
             cross_copy(s, n).start()
 
@@ -709,36 +718,69 @@
 
     @pl.when(inner == 1)
     def _():
+        pass_on(0, (0,))
         for step in far_steps[1:]:
             xg_copy(0, first, step).wait_send()
             xg_copy(1, first, step).wait_send()
-        reply(first, *far_part)
         arrive_across()
         process(0, half, 1)
         across_reply().start()
-        pass_on(0)
+        pass_on(0, range(1, PIECES))
+        reply(first, *far_part)
         arrive(second, turn, 1)
 
     arrive(second, *last_part)
     process(second, *far_part)
-    pl.when(inner == 1)(lambda: reply(second, turn, 1))
+
+    @pl.when(inner == 1)
+    def _():
+        pass_on(1, range(PIECES))
+        reply(second, turn, 1)
+
     reply(second, *last_part)
-
-    @pl.when(inner == 1)
-    def _():
-        pass_on(1)
-        exchange(0, False, half + 1)
+    pl.when(inner == 1)(lambda: exchange(0, False, half + 1))
 
     @pl.when(outer)
     def _():
         exchange(1, False, half)
         for t in others:
             rows_out(first, 1, t)
-        pass_on(0)
-        pass_on(1)
+        pass_on(0, range(PIECES))
+        pass_on(1, range(PIECES))
 
     scatter(first, 0, half // 2, True)
     scatter(second, 0, half // 2)
+
+    for step in far_steps:
+        xg_copy(0, second, step).wait_send()
+        xg_copy(1, second, step).wait_send()
+
+    @pl.when(outer)
+    def _():
+        for step in far_steps:
+            xg_copy(0, first, step).wait_send()
+            xg_copy(1, first, step).wait_send()
+
+    @pl.when(inner == 1)
+    def _():
+        across_copy(0).wait_send()
+        across_copy(1).wait_send()
+
+    for f in range(2):
+        for step in near:
+            if step < turn:
+                xg_copy(0, f, step).wait_send()
+                xg_copy(1, f, step).wait_send()
+        for s in range(2):
+            for t in range(halves):
+                twin_copy(f, s, 2 * t + (1 - side), t).wait_send()
+    for m, n in pieces:
+        w_cross(m, n).wait_send()
+        for t in range(halves):
+            w_twin(m, n, t).wait_send()
+        for t in others:
+            w_row(m, n, t).wait_send()
+
     scatter(second, half // 2, half // 2)
     for s, out in enumerate((dwo, dwi)):
         for n in range(PIECES):
@@ -746,49 +788,26 @@
     scatter(first, half // 2, half // 2)
     for h in range(heads):
         dx[:, pl.ds(h * sub, sub)] = acc[pl.ds(h * tokens, tokens), :].astype(BF16)
+
+    @pl.when(inner == 1)
+    def _():
+        across_reply().wait_send()
+        r_copy(second, turn).wait_send()
+
+    r_copy(first, turn).wait_send()
+    for f in range(2):
+        for step in near:
+            if step != turn:
+                r_copy(f, step).wait_send()
+        for s in range(2):
+            for t in others:
+                for n in range(PIECES):
+                    row_copy(f, s, t, n).wait_send()
     for s, (out, got) in enumerate(((dwo, gpo), (dwi, gpi))):
         for n in range(PIECES):
             landed(got.at[cut(s, n)], c_recv.at[s, n]).wait()
             out[0, cut(s, n)] = out[0, cut(s, n)] + got[cut(s, n)].astype(F32)
 
-    for step in far_steps:
-        xg_copy(0, second, step).wait_send()
-        xg_copy(1, second, step).wait_send()
-
-    @pl.when(outer)
-    def _():
-        for step in far_steps:
-            xg_copy(0, first, step).wait_send()
-            xg_copy(1, first, step).wait_send()
-        r_copy(first, turn).wait_send()
-
-    @pl.when(inner == 1)
-    def _():
-        across_copy(0).wait_send()
-        across_copy(1).wait_send()
-        across_reply().wait_send()
-        r_copy(first, turn).wait_send()
-        r_copy(second, turn).wait_send()
-
-    for f in range(2):
-        for step in near:
-            if step < turn:
-                xg_copy(0, f, step).wait_send()
-                xg_copy(1, f, step).wait_send()
-            if step != turn:
-                r_copy(f, step).wait_send()
-        for s in range(2):
-            for t in range(halves):
-                twin_copy(f, s, 2 * t + (1 - side), t).wait_send()
-            for t in others:
-                for n in range(PIECES):
-                    row_copy(f, s, t, n).wait_send()
-    for m, n in pieces:
-        w_cross(m, n).wait_send()
-        for t in range(halves):
-            w_twin(m, n, t).wait_send()
-        for t in others:
-            w_row(m, n, t).wait_send()
     for s in range(2):
         for n in range(PIECES):
             cross_copy(s, n).wait_send()
@@ -842,9 +861,12 @@
     results = pl.pallas_call(
         functools.partial(paired, dims),
         out_shape=tuple(pltpu.VMEM(shape, kind) for shape, kind in shapes),
-        in_specs=[vmem, vmem, vmem, any_spec, any_spec, any_spec, any_spec, any_spec],
+        in_specs=[any_spec] * 8,
         out_specs=(vmem, vmem, vmem, vmem),
         scratch_shapes=[
+            pltpu.VMEM((top, rows), jnp.int32),
+            pltpu.VMEM((top, rows), jnp.int32),
+            pltpu.VMEM((top, rows), F32),
             pltpu.VMEM((top, rows), jnp.int32),
             pltpu.VMEM((rows, sub), BF16),
             pltpu.VMEM((rows, sub), BF16),
@@ -860,7 +882,7 @@
             *[pltpu.VMEM((part_out, sub), BF16), pltpu.VMEM((part, ff), BF16)] * 2,
             pltpu.VMEM((tokens, heads, top, sub), BF16),
             pltpu.VMEM((tokens, 128), F32),
-            dma((2 * heads + 3,)),
+            dma((2 * heads + 6,)),
             *[dma((2, 2, half))] * 2,
             *[dma((2, half))] * 2,
             *[dma((2, PIECES))] * 2,

time: 124 us -> 122 us (0.984)
  Pallas kernels: 123 us -> 121 us
    pallas_call x1, Pallas kernels: 121 us -> 119 us  [paired_call(): pl.pallas_call(functools.partial(paired, dims), out_shape=tuple((pltpu.VM...]
where the time goes in v5:
time: 122 us
  Pallas kernels  121 us (99%)
    pallas_call x1, Pallas kernels, paired_call(): pl.pallas_call(functools.partial(paired, dims), out_shape=tuple((pltpu.VM...  119 us

profile of v5, /device:TPU:0, one launch (start us, length us, event | category | flops | bytes accessed | tf_op | source)
XLA Modules:
  0.0 121.8 jit_solution(3859975974023280985)
XLA Ops:
  0.6 119.3 %shard_map.111 = (bf16[128,4096]{1,0:T(8,128)(2,1)S(1)}, f32[1,256,1024]{2,1,0:T(8,128)S(1)}, f32[1,256,1024]{2,1,0:T(8,128)S(1)}, f32[2,512]{1,0:T(2,128)S(1)}) custom-call(s32[2,512]{1,0:T(2,128)} %bitcast.12, s32[2,512]{1,0:T(2,128)} %bitcast.13, f32[2,512]{1,0:T(2,128)} %bitcast.14, bf16[128,4096]{1,0:T(8,128)(2,1)} %x_hbm.1, bf16[128,4096]{1,0:T(8,128)(2,1)} %g_hbm.1, ...), custom_call_target="tpu_custom_call" | custom-call | flops 20000000000 | bytes 16777216 | tf_op jit(solution)/shard_map/pallas_call | solution.py:861
  119.9 1.7 %shard_map.112 = (bf16[128,4096]{1,0:T(8,128)(2,1)}, f32[1,256,1024]{2,1,0:T(8,128)}, f32[1,256,1024]{2,1,0:T(8,128)}, f32[2,512]{1,0:T(2,128)}) custom-call(bf16[128,4096]{1,0:T(8,128)(2,1)S(1)} %get-tuple-element.12.refs_0_, f32[1,256,1024]{2,1,0:T(8,128)S(1)} %get-tuple-element.13.refs_1_, f32[1,256,1024]{2,1,0:T(8,128)S(1)} %get-tuple-element.14.refs_2_, ...), custom_call_target="tpu_custom_call" | custom-call | tf_op jit(solution)/shard_map/pallas_call | solution.py:904

commit v6 on v5

--- a/solution.py
+++ b/solution.py
@@ -332,6 +332,7 @@
 
 
 PIECES = 2
+WEIGHT_PIECES = 4
 
 
 def paired(
@@ -411,25 +412,28 @@
         return base + partner(low, s, half)
 
     def part_of(m, quarter, n):
-        size = (sub, ff)[m] // replicas // PIECES
-        return rows_of(quarter * PIECES + n, size)
+        size = (sub, ff)[m] // replicas // WEIGHT_PIECES
+        return rows_of(quarter * WEIGHT_PIECES + n, size)
 
     def held(m, quarter, n):
         return (win, wout)[m].at[1, part_of(m, quarter, n)]
+
+    def rows_held(m, quarters):
+        return (win, wout)[m].at[1, pl.ds(0, quarters * ((sub, ff)[m] // replicas))]
 
     def w_cross(m, n):
         return remote(
             (win_hbm, wout_hbm)[m].at[0, part_of(m, mine, n)], held(m, mine, n),
-            wz_send.at[m, n], wz_recv.at[m, n], {"expert": opposite},
+            wz_send.at[m], wz_recv.at[m, n], {"expert": opposite},
         )
 
     def w_twin(m, n, t):
         ref = held(m, 2 * t + side, n)
-        return remote(ref, ref, wt_send.at[m, n, t], wt_recv.at[m, n, t], {"dp": twin})
+        return remote(ref, ref, wt_send.at[m], wt_recv.at[m], {"dp": twin})
 
     def w_row(m, n, t):
         ref = held(m, mine, n)
-        return remote(ref, ref, wy_send.at[m, n, t], wy_recv.at[m, n, row], {"dp": 2 * t + side})
+        return remote(ref, ref, wy_send.at[m], wy_recv.at[m, n, row], {"dp": 2 * t + side})
 
     def xg_copy(s, f, step):
         src, dst = ((sx, rx), (sg, rg))[s]
@@ -457,7 +461,7 @@
 
     def twin_copy(f, s, q, t):
         src, dst = ((po, tpo), (pi, tpi))[s]
-        return remote(src.at[f, q], dst.at[f, t], t_send.at[f, s, t], t_recv.at[f, s, t], {"dp": twin})
+        return remote(src.at[f, q], dst.at[f, t], t_send.at[s], t_recv.at[f, s, t], {"dp": twin})
 
     def cut(s, n):
         size = (dwo, dwi)[s].shape[1] // PIECES
@@ -467,16 +471,16 @@
         src, dst = ((so, rpo), (si, rpi))[s]
         return remote(
             src.at[f, t, cut(s, n)], dst.at[f, row, cut(s, n)],
-            y_send.at[f, s, n, t], y_recv.at[f, s, n, row], {"dp": 2 * t + side},
+            y_send.at[s], y_recv.at[f, s, n, row], {"dp": 2 * t + side},
         )
 
     def cross_copy(s, n):
         src, dst = ((cpo, gpo), (cpi, gpi))[s]
         return remote(
-            src.at[cut(s, n)], dst.at[cut(s, n)], c_send.at[s, n], c_recv.at[s, n], {"expert": opposite}
-        )
-
-    pieces = [(m, n) for m in range(2) for n in range(PIECES)]
+            src.at[cut(s, n)], dst.at[cut(s, n)], c_send.at[s], c_recv.at[s, n], {"expert": opposite}
+        )
+
+    pieces = [(m, n) for m in range(2) for n in range(WEIGHT_PIECES)]
 
     @pl.when(outer)
     def _():
@@ -580,6 +584,13 @@
             if before is not None:
                 from_rows(*before)
             before = (m, n)
+            if before == pieces[-2]:
+
+                @pl.when(inner == 1)
+                def _():
+                    for piece in pieces:
+                        w_cross(*piece).start()
+
             if before == pieces[-1]:
 
                 @pl.when(outer)
@@ -587,15 +598,9 @@
                     for t in others:
                         rows_out(first, 0, t)
 
-                @pl.when(inner == 1)
-                def _():
-                    for piece in pieces:
-                        w_cross(*piece).start()
-
         from_rows(*before)
-        for m, n in pieces:
-            for t in range(halves):
-                landed(held(m, 2 * t + (1 - side), n), wt_recv.at[m, n, t]).wait()
+        for m in range(2):
+            landed(rows_held(m, halves), wt_recv.at[m]).wait()
 
     def arrive(f, s, n):
         for step in range(s, s + n):
@@ -771,15 +776,11 @@
             if step < turn:
                 xg_copy(0, f, step).wait_send()
                 xg_copy(1, f, step).wait_send()
-        for s in range(2):
-            for t in range(halves):
-                twin_copy(f, s, 2 * t + (1 - side), t).wait_send()
-    for m, n in pieces:
-        w_cross(m, n).wait_send()
-        for t in range(halves):
-            w_twin(m, n, t).wait_send()
-        for t in others:
-            w_row(m, n, t).wait_send()
+    for m in range(2):
+        landed(rows_held(m, 1), wz_send.at[m]).wait()
+        landed(rows_held(m, halves), wt_send.at[m]).wait()
+        landed(rows_held(m, halves - 1), wy_send.at[m]).wait()
+        landed((po, pi)[m].at[0], t_send.at[m]).wait()
 
     scatter(second, half // 2, half // 2)
     for s, out in enumerate((dwo, dwi)):
@@ -799,18 +800,15 @@
         for step in near:
             if step != turn:
                 r_copy(f, step).wait_send()
-        for s in range(2):
-            for t in others:
-                for n in range(PIECES):
-                    row_copy(f, s, t, n).wait_send()
+    for s in range(2):
+        landed((po, pi)[s].at[0, pl.ds(0, 2 * (halves - 1))], y_send.at[s]).wait()
     for s, (out, got) in enumerate(((dwo, gpo), (dwi, gpi))):
         for n in range(PIECES):
             landed(got.at[cut(s, n)], c_recv.at[s, n]).wait()
             out[0, cut(s, n)] = out[0, cut(s, n)] + got[cut(s, n)].astype(F32)
 
     for s in range(2):
-        for n in range(PIECES):
-            cross_copy(s, n).wait_send()
+        landed((cpo, cpi)[s], c_send.at[s]).wait()
 
 
 def put_out(*refs):
@@ -885,11 +883,18 @@
             dma((2 * heads + 6,)),
             *[dma((2, 2, half))] * 2,
             *[dma((2, half))] * 2,
-            *[dma((2, PIECES))] * 2,
-            *[dma((2, PIECES, halves))] * 4,
-            *[dma((2, 2, halves))] * 2,
-            *[dma((2, 2, PIECES, halves))] * 2,
-            *[dma((2, PIECES))] * 2,
+            dma((2,)),
+            dma((2, WEIGHT_PIECES)),
+            dma((2,)),
+            dma((2,)),
+            dma((2,)),
+            dma((2, WEIGHT_PIECES, halves)),
+            dma((2,)),
+            dma((2, 2, halves)),
+            dma((2,)),
+            dma((2, 2, PIECES, halves)),
+            dma((2,)),
+            dma((2, PIECES)),
             dma((3,)),
             dma((2,)),
         ],

time: 122 us -> 122 us (level)
  no operation moved by 1% of the time
where the time goes in v6:
time: 122 us
  Pallas kernels  121 us (99%)
    pallas_call x1, Pallas kernels, paired_call(): pl.pallas_call(functools.partial(paired, dims), out_shape=tuple((pltpu.VM...  119 us

profile of v6, /device:TPU:0, one launch (start us, length us, event | category | flops | bytes accessed | tf_op | source)
XLA Modules:
  0.0 121.5 jit_solution(11440973654024000062)
XLA Ops:
  0.6 119.0 %shard_map.111 = (bf16[128,4096]{1,0:T(8,128)(2,1)S(1)}, f32[1,256,1024]{2,1,0:T(8,128)S(1)}, f32[1,256,1024]{2,1,0:T(8,128)S(1)}, f32[2,512]{1,0:T(2,128)S(1)}) custom-call(s32[2,512]{1,0:T(2,128)} %bitcast.12, s32[2,512]{1,0:T(2,128)} %bitcast.13, f32[2,512]{1,0:T(2,128)} %bitcast.14, bf16[128,4096]{1,0:T(8,128)(2,1)} %x_hbm.1, bf16[128,4096]{1,0:T(8,128)(2,1)} %g_hbm.1, ...), custom_call_target="tpu_custom_call" | custom-call | flops 20000000000 | bytes 16777216 | tf_op jit(solution)/shard_map/pallas_call | solution.py:859
  119.7 1.7 %shard_map.112 = (bf16[128,4096]{1,0:T(8,128)(2,1)}, f32[1,256,1024]{2,1,0:T(8,128)}, f32[1,256,1024]{2,1,0:T(8,128)}, f32[2,512]{1,0:T(2,128)}) custom-call(bf16[128,4096]{1,0:T(8,128)(2,1)S(1)} %get-tuple-element.12.refs_0_, f32[1,256,1024]{2,1,0:T(8,128)S(1)} %get-tuple-element.13.refs_1_, f32[1,256,1024]{2,1,0:T(8,128)S(1)} %get-tuple-element.14.refs_2_, ...), custom_call_target="tpu_custom_call" | custom-call | tf_op jit(solution)/shard_map/pallas_call | solution.py:909
